TPU v7x, 32 devices: a whole 2x2x4 slice. The times are simulated.
32 devices in a mesh: gx: 4 (over y, x), gy: 2 (over core), gz: 4 (over z).
Axes of the slice: x: 2, y: 2, z: 4, core: 2. Of those that a mesh axis runs over, the one named last changes fastest.
Arguments:
- right_side: float32 [8, 32, 64, 512], P(None, 'gx', 'gy', 'gz'), may hold values from -12 to 12
- shift: float32 [32, 64, 512], P('gx', 'gy', 'gz'), may hold values from 0.02 to 2
Outputs:
- solution_block: float32 [8, 32, 64, 512], P(None, 'gx', 'gy', 'gz')
- residual_norms: float32 [8], replicated
All inputs are finite; a program needn't handle non-finite values.
Results may differ from a plain program's by a relative error of at most 0.0003.
Values sent between devices are 32-bit elements; how exact they have to be, the bound alone decides.
No kernel may reach another device: no remote copies, remote signals or barrier semaphores. Data moves between devices by JAX's collectives and lax.ppermute only.
A program may use at most 128 MiB of HBM per device.

v0:
```python
import jax
import jax.numpy as jnp
from jax import lax
from jax.sharding import PartitionSpec as P

ITERS = 2


def padded_2(block, sides, width):
    for axis, dim in sides:
        count = lax.axis_size(axis)
        forward = [(i, i + 1) for i in range(count - 1)]
        backward = [(target, source) for source, target in forward]
        low = lax.ppermute(
            lax.slice_in_dim(block, block.shape[dim] - width, None, axis=dim), axis, forward
        )
        high = lax.ppermute(lax.slice_in_dim(block, 0, width, axis=dim), axis, backward)
        block = jnp.concatenate([low, block, high], axis=dim)
    return block


def operate(fields, shift):
    padded = padded_2(fields, (("gx", 1), ("gy", 2), ("gz", 3)), 1)
    beside = padded[:, 2:, 1:-1, 1:-1] + padded[:, :-2, 1:-1, 1:-1]
    beside = beside + padded[:, 1:-1, 2:, 1:-1] + padded[:, 1:-1, :-2, 1:-1]
    beside = beside + padded[:, 1:-1, 1:-1, 2:] + padded[:, 1:-1, 1:-1, :-2]
    return (6.0 + shift)[None] * fields - beside


def lower_inverse(lower):
    count = lower.shape[0]
    return jax.scipy.linalg.solve_triangular(lower, jnp.eye(count, dtype=lower.dtype), lower=True)


def small_dot(left, right):
    return jnp.dot(left, right, precision=lax.Precision.HIGHEST)


def body(right_side, shift):
    width = right_side.shape[0]
    shape = right_side.shape
    rows = right_side.reshape(width, -1)
    gram = lax.psum(small_dot(rows, rows.T), ("gx", "gy", "gz"))
    lower = jnp.linalg.cholesky(gram)
    start_coeff = lower.T
    basis = [small_dot(lower_inverse(lower), rows)]
    hessen = jnp.zeros(((ITERS + 1) * width, ITERS * width), jnp.float32)
    for step in range(ITERS):
        image = operate(basis[step].reshape(shape), shift).reshape(width, -1)
        stacked = jnp.concatenate(basis, axis=0)
        products = lax.psum(
            small_dot(jnp.concatenate([stacked, image], axis=0), image.T), ("gx", "gy", "gz")
        )
        coeffs = products[:-width]
        gram = products[-width:] - small_dot(coeffs.T, coeffs)
        projected = image - small_dot(coeffs.T, stacked)
        lower = jnp.linalg.cholesky(gram)
        hessen = hessen.at[: (step + 1) * width, step * width : (step + 1) * width].set(coeffs)
        hessen = hessen.at[
            (step + 1) * width : (step + 2) * width, step * width : (step + 1) * width
        ].set(lower.T)
        if step + 1 < ITERS:
            basis.append(small_dot(lower_inverse(lower), projected))
    target = jnp.zeros(((ITERS + 1) * width, width), jnp.float32).at[:width].set(start_coeff)
    normal = small_dot(hessen.T, hessen)
    factor = jnp.linalg.cholesky(normal)
    coeff_y = jax.scipy.linalg.cho_solve((factor, True), small_dot(hessen.T, target))
    solution = small_dot(coeff_y.T, jnp.concatenate(basis, axis=0)).reshape(shape)
    leftover = target - small_dot(hessen, coeff_y)
    norms = jnp.sqrt(jnp.sum(leftover * leftover, axis=0))
    return (solution, norms)


def solution(mesh):
    in_specs = (P(None, "gx", "gy", "gz"), P("gx", "gy", "gz"))
    out_specs = (P(None, "gx", "gy", "gz"), P())
    return jax.shard_map(body, mesh=mesh, in_specs=in_specs, out_specs=out_specs, check_vma=False)
```

profile of v0, /device:TPU:0, one launch (start us, length us, event | category | flops | bytes accessed | tf_op | source)
XLA Modules:
  0.0 228.1 jit_solution(12695287434098205644)
XLA Ops:
  0.6 4.9 %convolution_bitcast_fusion = f32[8,8]{0,1:T(8,128)S(1)} fusion(f32[8,8,32,128]{3,2,1,0:T(8,128)} %param.15), kind=kOutput, calls=%fused_computation.19 | convolution fusion | flops 25165824 | bytes 1048832 | tf_op jit(solution)/shard_map/dot_general | solution.py:36
  5.5 42.0 %psum.21 = f32[8,8]{0,1:T(8,128)S(1)} all-reduce(f32[8,8]{0,1:T(8,128)S(1)} %convolution_bitcast_fusion), channel_id=1, replica_groups=mesh['gx'=4,'gy'=2,'gz'=4] {'gx','gy','gz'}, use_global_device_ids=true, to_apply=%region_0.0 | all-reduce | flops 64 | bytes 512 | tf_op jit(solution)/shard_map/psum | solution.py:43
  47.5 0.7 cholesky.94
  50.4 1.5 fusion.12
  51.9 1.3 collective-permute-start
  53.2 4.8 %collective-permute-start.1 = (f32[8,1,32,128]{3,0,2,1:T(8,128)S(1)}, f32[8,1,32,128]{3,0,2,1:T(8,128)S(1)}, u32[]{:S(2)}, u32[]{:S(2)}) collective-permute-start(f32[8,1,32,128]{3,0,2,1:T(8,128)S(1)} %get-tuple-element.84), channel_id=1, source_target_pairs={{0,8},{8,16},{16,24},{1,9},{9,17},{17,25},{2,10},{10,18},{18,26},{... | collective-permute-start | bytes 393224 | tf_op jit(solution)/shard_map/ppermute | solution.py:14
  58.1 1.0 collective-permute-done
  59.1 1.5 collective-permute-done.1
  60.6 1.3 collective-permute-start.2
  61.9 3.0 %collective-permute-start.3 = (f32[8,10,1,128]{3,0,2,1:T(8,128)S(1)}, f32[8,10,1,128]{3,0,2,1:T(8,128)S(1)}, u32[]{:S(2)}, u32[]{:S(2)}) collective-permute-start(f32[8,10,1,128]{3,0,2,1:T(8,128)S(1)} %get-tuple-element.80), channel_id=1, source_target_pairs={{0,4},{1,5},{2,6},{3,7},{8,12},{9,13},{10,14},{11,15},{16,20},{17,... | collective-permute-start | bytes 122888 | tf_op jit(solution)/shard_map/ppermute | solution.py:14
  64.9 0.8 collective-permute-done.3
  66.4 1.5 fusion.56
  67.9 2.0 copy.130
  70.0 1.3 collective-permute-start.4
  71.2 0.7 copy.132
  71.9 4.5 %collective-permute-start.5 = (f32[8,10,34,1]{2,0,3,1:T(8,128)S(1)}, f32[8,10,34,1]{2,0,3,1:T(8,128)S(1)}, u32[]{:S(2)}, u32[]{:S(2)}) collective-permute-start(f32[8,10,34,1]{2,0,3,1:T(8,128)S(1)} %copy.132), channel_id=1, source_target_pairs={{0,1},{1,2},{2,3},{4,5},{5,6},{6,7},{8,9},{9,10},{10,11},{12,13},{... | collective-permute-start | bytes 32648 | tf_op jit(solution)/shard_map/ppermute | solution.py:14
  77.1 0.7 copy.131
  78.1 1.8 copy.133
  79.9 3.0 %fusion.22 = f32[8,8,32,128]{3,0,2,1:T(8,128)S(1)} fusion(f32[8,10,34,1]{3,0,2,1:T(8,128)} %copy.133, f32[8,10,1,128]{3,0,2,1:T(8,128)S(1)} %collective-permute-done.2, f32[8,10,1,128]{3,0,2,1:T(8,128)} %copy-done.6, f32[8,1,32,128]{3,0,2,1:T(8,128)} %copy-done.3, f32[8,8,32,128]{3,0,2,1:T(8,128)S(1)} %bitcast.73, f32[8,1,32,128]{3,0,2,1:T(8,128)} %copy-done.4, ...), kind=kLoop, calls=%fused_computation.50 | loop fusion | flops 6553600 | bytes 2594048 | tf_op jit(solution)/shard_map/sub | solution.py:27
  82.9 2.6 %fusion.6 = f32[16,8]{0,1:T(8,128)S(1)} fusion(f32[8,32768]{1,0:T(8,128)S(1)} %bitcast.78, f32[8,32768]{1,0:T(8,128)S(1)} %fusion.12), kind=kOutput, calls=%fused_computation.9 | convolution fusion | flops 50855936 | bytes 2097664 | tf_op jit(solution)/shard_map/dot_general | solution.py:36
  85.5 43.2 %psum.22 = f32[16,8]{0,1:T(8,128)S(1)} all-reduce(f32[16,8]{0,1:T(8,128)S(1)} %fusion.6), channel_id=1, replica_groups=mesh['gx'=4,'gy'=2,'gz'=4] {'gx','gy','gz'}, use_global_device_ids=true, to_apply=%region_3.0 | all-reduce | flops 128 | bytes 1024 | tf_op jit(solution)/shard_map/psum | solution.py:51
  128.6 1.0 convolution_subtract_fusion
  129.8 0.7 cholesky.105
  132.7 1.0 fusion.60
  133.7 1.3 collective-permute-start.6
  135.0 4.8 %collective-permute-start.7 = (f32[8,1,32,128]{3,0,2,1:T(8,128)S(1)}, f32[8,1,32,128]{3,0,2,1:T(8,128)S(1)}, u32[]{:S(2)}, u32[]{:S(2)}) collective-permute-start(f32[8,1,32,128]{3,0,2,1:T(8,128)S(1)} %get-tuple-element.82), channel_id=1, source_target_pairs={{0,8},{8,16},{16,24},{1,9},{9,17},{17,25},{2,10},{10,18},{18,26},{... | collective-permute-start | bytes 393224 | tf_op jit(solution)/shard_map/ppermute | solution.py:14
  139.9 1.2 collective-permute-done.6
  141.1 1.3 collective-permute-done.7
  142.4 1.3 collective-permute-start.8
  143.7 3.0 %collective-permute-start.9 = (f32[8,10,1,128]{3,0,2,1:T(8,128)S(1)}, f32[8,10,1,128]{3,0,2,1:T(8,128)S(1)}, u32[]{:S(2)}, u32[]{:S(2)}) collective-permute-start(f32[8,10,1,128]{3,0,2,1:T(8,128)S(1)} %get-tuple-element.78), channel_id=1, source_target_pairs={{0,4},{1,5},{2,6},{3,7},{8,12},{9,13},{10,14},{11,15},{16,20},{17,... | collective-permute-start | bytes 122888 | tf_op jit(solution)/shard_map/ppermute | solution.py:14
  146.7 0.8 collective-permute-done.9
  148.3 1.5 fusion.55
  149.8 2.6 %copy.137 = f32[8,10,34,1]{2,0,3,1:T(8,128)} copy(f32[8,10,34,1]{3,0,2,1:T(8,128)} %get-tuple-element.74) | data formatting | bytes 21760 | tf_op jit(solution)/shard_map/slice | solution.py:17
  152.4 1.3 collective-permute-start.10
  153.7 1.3 copy.139
  155.0 5.2 %collective-permute-start.11 = (f32[8,10,34,1]{2,0,3,1:T(8,128)}, f32[8,10,34,1]{2,0,3,1:T(8,128)}, u32[]{:S(2)}, u32[]{:S(2)}) collective-permute-start(f32[8,10,34,1]{2,0,3,1:T(8,128)} %copy.139), channel_id=1, source_target_pairs={{0,1},{1,2},{2,3},{4,5},{5,6},{6,7},{8,9},{9,10},{10,11},{12,13},{... | collective-permute-start | bytes 32648 | tf_op jit(solution)/shard_map/ppermute | solution.py:14
  161.8 1.5 copy.138
  163.3 2.6 %copy.140 = f32[8,10,34,1]{3,0,2,1:T(8,128)} copy(f32[8,10,34,1]{2,0,3,1:T(8,128)} %collective-permute-done.11) | data formatting | bytes 21760 | tf_op jit(solution)/shard_map/ppermute | solution.py:14
  165.8 3.0 %fusion.16 = f32[8,8,32,128]{3,0,2,1:T(8,128)S(1)} fusion(f32[8,10,34,1]{3,0,2,1:T(8,128)} %copy.140, f32[8,10,1,128]{3,0,2,1:T(8,128)S(1)} %collective-permute-done.8, f32[8,10,1,128]{3,0,2,1:T(8,128)} %copy-done.5, f32[8,1,32,128]{3,0,2,1:T(8,128)} %copy-done.1, f32[8,8,32,128]{3,0,2,1:T(8,128)S(1)} %bitcast.77, f32[8,1,32,128]{3,0,2,1:T(8,128)} %copy-done.2, ...), kind=kLoop, calls=%fused_computation.26 | loop fusion | flops 6553600 | bytes 2594048 | tf_op jit(solution)/shard_map/sub | solution.py:27
  168.9 3.0 %fusion = f32[24,8]{0,1:T(8,128)S(1)} fusion(f32[8,32768]{1,0:T(8,128)S(1)} %bitcast.82, f32[8,32768]{1,0:T(8,128)S(1)} %fusion.60, f32[8,32768]{1,0:T(8,128)S(1)} %fusion.12), kind=kOutput, calls=%fused_computation.1 | convolution fusion | flops 77070336 | bytes 3146496 | tf_op jit(solution)/shard_map/dot_general | solution.py:36
  171.9 42.0 %psum.23 = f32[24,8]{0,1:T(8,128)S(1)} all-reduce(f32[24,8]{0,1:T(8,128)S(1)} %fusion), channel_id=1, replica_groups=mesh['gx'=4,'gy'=2,'gz'=4] {'gx','gy','gz'}, use_global_device_ids=true, to_apply=%region_5.0 | all-reduce | flops 192 | bytes 1536 | tf_op jit(solution)/shard_map/psum | solution.py:51
  214.0 0.7 cholesky.116
  216.1 2.0 dynamic-slice_select_fusion
  218.1 1.7 scatter.20
  220.6 1.5 cholesky.41
  223.4 1.2 custom-call.15
  225.3 1.1 fusion.7
  227.0 1.2 copy.144
  (67 shorter events, 13.4 us)
Async XLA Ops:
  0.6 49.8 %copy-start = (f32[8,8,32,128]{3,2,1,0:T(8,128)S(1)}, f32[8,8,32,128]{3,2,1,0:T(8,128)}, u32[]{:S(2)}) copy-start(f32[8,8,32,128]{3,2,1,0:T(8,128)} %param.15) | copy-start | bytes 3145732
  51.9 7.1 %collective-permute-start = (f32[8,1,32,128]{3,0,2,1:T(8,128)S(1)}, f32[8,1,32,128]{3,0,2,1:T(8,128)S(1)}, u32[]{:S(2)}, u32[]{:S(2)}) collective-permute-start(f32[8,1,32,128]{3,0,2,1:T(8,128)S(1)} %get-tuple-element.85), channel_id=1, source_target_pairs={{8,0},{16,8},{24,16},{9,1},{17,9},{25,17},{10,2},{18,10},{26,18},{... | collective-permute-start | bytes 393224 | tf_op jit(solution)/shard_map/ppermute | solution.py:17
  53.2 7.3 %collective-permute-start.1 = (f32[8,1,32,128]{3,0,2,1:T(8,128)S(1)}, f32[8,1,32,128]{3,0,2,1:T(8,128)S(1)}, u32[]{:S(2)}, u32[]{:S(2)}) collective-permute-start(f32[8,1,32,128]{3,0,2,1:T(8,128)S(1)} %get-tuple-element.84), channel_id=1, source_target_pairs={{0,8},{8,16},{16,24},{1,9},{9,17},{17,25},{2,10},{10,18},{18,26},{... | collective-permute-start | bytes 393224 | tf_op jit(solution)/shard_map/ppermute | solution.py:14
  59.1 6.8 %copy-start.3 = (f32[8,1,32,128]{3,0,2,1:T(8,128)}, f32[8,1,32,128]{3,0,2,1:T(8,128)S(1)}, u32[]{:S(2)}) copy-start(f32[8,1,32,128]{3,0,2,1:T(8,128)S(1)} %collective-permute-done) | copy-start | bytes 393220
  60.6 5.3 %copy-start.4 = (f32[8,1,32,128]{3,0,2,1:T(8,128)}, f32[8,1,32,128]{3,0,2,1:T(8,128)S(1)}, u32[]{:S(2)}) copy-start(f32[8,1,32,128]{3,0,2,1:T(8,128)S(1)} %collective-permute-done.1) | copy-start | bytes 393220
  60.6 4.3 %collective-permute-start.2 = (f32[8,10,1,128]{3,0,2,1:T(8,128)S(1)}, f32[8,10,1,128]{3,0,2,1:T(8,128)S(1)}, u32[]{:S(2)}, u32[]{:S(2)}) collective-permute-start(f32[8,10,1,128]{3,0,2,1:T(8,128)S(1)} %get-tuple-element.81), channel_id=1, source_target_pairs={{4,0},{5,1},{6,2},{7,3},{12,8},{13,9},{14,10},{15,11},{20,16},{21,... | collective-permute-start | bytes 122888 | tf_op jit(solution)/shard_map/ppermute | solution.py:17
  61.9 3.9 %collective-permute-start.3 = (f32[8,10,1,128]{3,0,2,1:T(8,128)S(1)}, f32[8,10,1,128]{3,0,2,1:T(8,128)S(1)}, u32[]{:S(2)}, u32[]{:S(2)}) collective-permute-start(f32[8,10,1,128]{3,0,2,1:T(8,128)S(1)} %get-tuple-element.80), channel_id=1, source_target_pairs={{0,4},{1,5},{2,6},{3,7},{8,12},{9,13},{10,14},{11,15},{16,20},{17,... | collective-permute-start | bytes 122888 | tf_op jit(solution)/shard_map/ppermute | solution.py:14
  65.8 0.6 copy-start.6
  67.9 8.5 %copy-start.7 = (f32[8,32,128]{2,1,0:T(8,128)S(1)}, f32[8,32,128]{2,1,0:T(8,128)}, u32[]{:S(2)}) copy-start(f32[8,32,128]{2,1,0:T(8,128)} %param.16) | copy-start | bytes 393220
  70.0 7.2 %collective-permute-start.4 = (f32[8,10,34,1]{2,0,3,1:T(8,128)S(1)}, f32[8,10,34,1]{2,0,3,1:T(8,128)S(1)}, u32[]{:S(2)}, u32[]{:S(2)}) collective-permute-start(f32[8,10,34,1]{2,0,3,1:T(8,128)S(1)} %copy.130), channel_id=1, source_target_pairs={{1,0},{2,1},{3,2},{5,4},{6,5},{7,6},{9,8},{10,9},{11,10},{13,12},{... | collective-permute-start | bytes 32648 | tf_op jit(solution)/shard_map/ppermute | solution.py:17
  71.9 6.2 %collective-permute-start.5 = (f32[8,10,34,1]{2,0,3,1:T(8,128)S(1)}, f32[8,10,34,1]{2,0,3,1:T(8,128)S(1)}, u32[]{:S(2)}, u32[]{:S(2)}) collective-permute-start(f32[8,10,34,1]{2,0,3,1:T(8,128)S(1)} %copy.132), channel_id=1, source_target_pairs={{0,1},{1,2},{2,3},{4,5},{5,6},{6,7},{8,9},{9,10},{10,11},{12,13},{... | collective-permute-start | bytes 32648 | tf_op jit(solution)/shard_map/ppermute | solution.py:14
  133.7 7.3 %collective-permute-start.6 = (f32[8,1,32,128]{3,0,2,1:T(8,128)S(1)}, f32[8,1,32,128]{3,0,2,1:T(8,128)S(1)}, u32[]{:S(2)}, u32[]{:S(2)}) collective-permute-start(f32[8,1,32,128]{3,0,2,1:T(8,128)S(1)} %get-tuple-element.83), channel_id=1, source_target_pairs={{8,0},{16,8},{24,16},{9,1},{17,9},{25,17},{10,2},{18,10},{26,18},{... | collective-permute-start | bytes 393224 | tf_op jit(solution)/shard_map/ppermute | solution.py:17
  135.0 7.3 %collective-permute-start.7 = (f32[8,1,32,128]{3,0,2,1:T(8,128)S(1)}, f32[8,1,32,128]{3,0,2,1:T(8,128)S(1)}, u32[]{:S(2)}, u32[]{:S(2)}) collective-permute-start(f32[8,1,32,128]{3,0,2,1:T(8,128)S(1)} %get-tuple-element.82), channel_id=1, source_target_pairs={{0,8},{8,16},{16,24},{1,9},{9,17},{17,25},{2,10},{10,18},{18,26},{... | collective-permute-start | bytes 393224 | tf_op jit(solution)/shard_map/ppermute | solution.py:14
  141.1 6.5 %copy-start.1 = (f32[8,1,32,128]{3,0,2,1:T(8,128)}, f32[8,1,32,128]{3,0,2,1:T(8,128)S(1)}, u32[]{:S(2)}) copy-start(f32[8,1,32,128]{3,0,2,1:T(8,128)S(1)} %collective-permute-done.6) | copy-start | bytes 393220
  142.4 5.2 %copy-start.2 = (f32[8,1,32,128]{3,0,2,1:T(8,128)}, f32[8,1,32,128]{3,0,2,1:T(8,128)S(1)}, u32[]{:S(2)}) copy-start(f32[8,1,32,128]{3,0,2,1:T(8,128)S(1)} %collective-permute-done.7) | copy-start | bytes 393220
  142.4 4.4 %collective-permute-start.8 = (f32[8,10,1,128]{3,0,2,1:T(8,128)S(1)}, f32[8,10,1,128]{3,0,2,1:T(8,128)S(1)}, u32[]{:S(2)}, u32[]{:S(2)}) collective-permute-start(f32[8,10,1,128]{3,0,2,1:T(8,128)S(1)} %get-tuple-element.79), channel_id=1, source_target_pairs={{4,0},{5,1},{6,2},{7,3},{12,8},{13,9},{14,10},{15,11},{20,16},{21,... | collective-permute-start | bytes 122888 | tf_op jit(solution)/shard_map/ppermute | solution.py:17
  143.7 3.9 %collective-permute-start.9 = (f32[8,10,1,128]{3,0,2,1:T(8,128)S(1)}, f32[8,10,1,128]{3,0,2,1:T(8,128)S(1)}, u32[]{:S(2)}, u32[]{:S(2)}) collective-permute-start(f32[8,10,1,128]{3,0,2,1:T(8,128)S(1)} %get-tuple-element.78), channel_id=1, source_target_pairs={{0,4},{1,5},{2,6},{3,7},{8,12},{9,13},{10,14},{11,15},{16,20},{17,... | collective-permute-start | bytes 122888 | tf_op jit(solution)/shard_map/ppermute | solution.py:14
  147.6 0.6 copy-start.5
  152.4 9.4 %collective-permute-start.10 = (f32[8,10,34,1]{2,0,3,1:T(8,128)}, f32[8,10,34,1]{2,0,3,1:T(8,128)}, u32[]{:S(2)}, u32[]{:S(2)}) collective-permute-start(f32[8,10,34,1]{2,0,3,1:T(8,128)} %copy.137), channel_id=1, source_target_pairs={{1,0},{2,1},{3,2},{5,4},{6,5},{7,6},{9,8},{10,9},{11,10},{13,12},{... | collective-permute-start | bytes 32648 | tf_op jit(solution)/shard_map/ppermute | solution.py:17
  155.0 8.3 %collective-permute-start.11 = (f32[8,10,34,1]{2,0,3,1:T(8,128)}, f32[8,10,34,1]{2,0,3,1:T(8,128)}, u32[]{:S(2)}, u32[]{:S(2)}) collective-permute-start(f32[8,10,34,1]{2,0,3,1:T(8,128)} %copy.139), channel_id=1, source_target_pairs={{0,1},{1,2},{2,3},{4,5},{5,6},{6,7},{8,9},{9,10},{10,11},{12,13},{... | collective-permute-start | bytes 32648 | tf_op jit(solution)/shard_map/ppermute | solution.py:14
where the time goes:
time: 229 us; the launch traced here: 228 us
  blocking collectives  127 us (55%)
  starting transfers between devices  33.1 us (14%)
  local copies, waits for them, and re-layouts  22.6 us (10%)
  other arithmetic  21 us (9%)
  matrix products  16.4 us (7%)
  waiting for transfers between devices  6.95 us (3%)
    psum x2, blocking collectives, body(): lax.psum(small_dot(jnp.concatenate([stacked, image], axis=0), image.T), (...  85.1 us
    psum x1, blocking collectives, body(): gram = lax.psum(small_dot(rows, rows.T), ('gx', 'gy', 'gz'))  42 us
    ppermute x6, starting transfers between devices, padded_2(): lax.ppermute(lax.slice_in_dim(block, block.shape[dim] - width, None, axis...  25.4 us
    dot_general x12, matrix products, small_dot(): return jnp.dot(left, right, precision=lax.Precision.HIGHEST)  15.7 us
    ppermute x6, starting transfers between devices, padded_2(): lax.ppermute(lax.slice_in_dim(block, 0, width, axis=dim), axis, backward)  7.73 us
    slice x4, local copies, waits for them, and re-layouts, padded_2(): lax.slice_in_dim(block, 0, width, axis=dim)  7.72 us
    sub x2, other arithmetic, operate(): return (6.0 + shift)[None] * fields - beside  6.01 us
    ppermute x6, waiting for transfers between devices, padded_2(): lax.ppermute(lax.slice_in_dim(block, block.shape[dim] - width, None, axis...  4.75 us
  transfers between devices with their start and end apart: 12, of which 7 were waited for; matrix products, arithmetic and copies ran while one was open for 3% of the time, Pallas kernels for 0%

commit v1 on v0

--- a/solution.py
+++ b/solution.py
@@ -48,8 +48,11 @@
     for step in range(ITERS):
         image = operate(basis[step].reshape(shape), shift).reshape(width, -1)
         stacked = jnp.concatenate(basis, axis=0)
-        products = lax.psum(
-            small_dot(jnp.concatenate([stacked, image], axis=0), image.T), ("gx", "gy", "gz")
+        products = jnp.sum(
+            lax.all_gather(
+                small_dot(jnp.concatenate([stacked, image], axis=0), image.T), ("gx", "gy", "gz")
+            ),
+            axis=0,
         )
         coeffs = products[:-width]
         gram = products[-width:] - small_dot(coeffs.T, coeffs)

time: 229 us -> 279 us (1.22)
  blocking collectives: 127 us -> 177 us
    all_gather x0 -> x2, blocking collectives: none -> 135 us  [body(): lax.all_gather(small_dot(jnp.concatenate([stacked, image], axis=0), image...]
    psum x2 -> x0, blocking collectives: 85.1 us -> none  [body(): lax.psum(small_dot(jnp.concatenate([stacked, image], axis=0), image.T), (...]
  transfers between devices with their start and end apart: 12 -> 12, of which waited for: 7 -> 7; matrix products, arithmetic and copies ran while one was open for 3% -> 2% of each run, Pallas kernels for 0% -> 0%
where the time goes in v1:
time: 279 us; the launch traced here: 278 us
  blocking collectives  177 us (63%)
  starting transfers between devices  32.9 us (12%)
  local copies, waits for them, and re-layouts  22.6 us (8%)
  other arithmetic  21.1 us (8%)
  matrix products  16.1 us (6%)
  waiting for transfers between devices  6.95 us (2%)
    all_gather x2, blocking collectives, body(): lax.all_gather(small_dot(jnp.concatenate([stacked, image], axis=0), image...  135 us
    psum x1, blocking collectives, body(): gram = lax.psum(small_dot(rows, rows.T), ('gx', 'gy', 'gz'))  42 us
    ppermute x6, starting transfers between devices, padded_2(): lax.ppermute(lax.slice_in_dim(block, block.shape[dim] - width, None, axis...  25.1 us
    dot_general x12, matrix products, small_dot(): return jnp.dot(left, right, precision=lax.Precision.HIGHEST)  15.5 us
    ppermute x6, starting transfers between devices, padded_2(): lax.ppermute(lax.slice_in_dim(block, 0, width, axis=dim), axis, backward)  7.73 us
    slice x4, local copies, waits for them, and re-layouts, padded_2(): lax.slice_in_dim(block, 0, width, axis=dim)  7.72 us
    sub x2, other arithmetic, operate(): return (6.0 + shift)[None] * fields - beside  6.01 us
  transfers between devices with their start and end apart: 12, of which 7 were waited for; matrix products, arithmetic and copies ran while one was open for 2% of the time, Pallas kernels for 0%

profile of v1, /device:TPU:0, one launch (start us, length us, event | category | flops | bytes accessed | tf_op | source)
XLA Modules:
  0.0 278.0 jit_solution(10991202681598207511)
XLA Ops:
  0.6 4.6 %convolution_bitcast_fusion = f32[8,8]{0,1:T(8,128)S(1)} fusion(f32[8,8,32,128]{3,2,1,0:T(8,128)} %param.15), kind=kOutput, calls=%fused_computation.21 | convolution fusion | flops 25165824 | bytes 1048832 | tf_op jit(solution)/shard_map/dot_general | solution.py:36
  5.2 42.0 %psum.7 = f32[8,8]{0,1:T(8,128)S(1)} all-reduce(f32[8,8]{0,1:T(8,128)S(1)} %convolution_bitcast_fusion), channel_id=1, replica_groups=mesh['gx'=4,'gy'=2,'gz'=4] {'gx','gy','gz'}, use_global_device_ids=true, to_apply=%region_0.0 | all-reduce | flops 64 | bytes 512 | tf_op jit(solution)/shard_map/psum | solution.py:43
  47.3 0.7 cholesky.94
  50.2 1.5 fusion.16
  51.7 1.3 collective-permute-start
  53.0 4.8 %collective-permute-start.1 = (f32[8,1,32,128]{3,0,2,1:T(8,128)S(1)}, f32[8,1,32,128]{3,0,2,1:T(8,128)S(1)}, u32[]{:S(2)}, u32[]{:S(2)}) collective-permute-start(f32[8,1,32,128]{3,0,2,1:T(8,128)S(1)} %get-tuple-element.84), channel_id=1, source_target_pairs={{0,8},{8,16},{16,24},{1,9},{9,17},{17,25},{2,10},{10,18},{18,26},{... | collective-permute-start | bytes 393224 | tf_op jit(solution)/shard_map/ppermute | solution.py:14
  57.8 1.0 collective-permute-done
  58.8 1.5 collective-permute-done.1
  60.3 1.3 collective-permute-start.2
  61.6 3.0 %collective-permute-start.3 = (f32[8,10,1,128]{3,0,2,1:T(8,128)S(1)}, f32[8,10,1,128]{3,0,2,1:T(8,128)S(1)}, u32[]{:S(2)}, u32[]{:S(2)}) collective-permute-start(f32[8,10,1,128]{3,0,2,1:T(8,128)S(1)} %get-tuple-element.80), channel_id=1, source_target_pairs={{0,4},{1,5},{2,6},{3,7},{8,12},{9,13},{10,14},{11,15},{16,20},{17,... | collective-permute-start | bytes 122888 | tf_op jit(solution)/shard_map/ppermute | solution.py:14
  64.7 0.8 collective-permute-done.3
  66.1 1.5 fusion.60
  67.7 2.0 copy.130
  69.7 1.3 collective-permute-start.4
  71.0 0.7 copy.132
  71.7 4.5 %collective-permute-start.5 = (f32[8,10,34,1]{2,0,3,1:T(8,128)S(1)}, f32[8,10,34,1]{2,0,3,1:T(8,128)S(1)}, u32[]{:S(2)}, u32[]{:S(2)}) collective-permute-start(f32[8,10,34,1]{2,0,3,1:T(8,128)S(1)} %copy.132), channel_id=1, source_target_pairs={{0,1},{1,2},{2,3},{4,5},{5,6},{6,7},{8,9},{9,10},{10,11},{12,13},{... | collective-permute-start | bytes 32648 | tf_op jit(solution)/shard_map/ppermute | solution.py:14
  76.9 0.7 copy.131
  77.9 1.8 copy.133
  79.6 3.0 %fusion.26 = f32[8,8,32,128]{3,0,2,1:T(8,128)S(1)} fusion(f32[8,10,34,1]{3,0,2,1:T(8,128)} %copy.133, f32[8,10,1,128]{3,0,2,1:T(8,128)S(1)} %collective-permute-done.2, f32[8,10,1,128]{3,0,2,1:T(8,128)} %copy-done.6, f32[8,1,32,128]{3,0,2,1:T(8,128)} %copy-done.3, f32[8,8,32,128]{3,0,2,1:T(8,128)S(1)} %bitcast.77, f32[8,1,32,128]{3,0,2,1:T(8,128)} %copy-done.4, ...), kind=kLoop, calls=%fused_computation.52 | loop fusion | flops 6553600 | bytes 2594048 | tf_op jit(solution)/shard_map/sub | solution.py:27
  82.7 2.6 fusion.10
  85.2 70.5 %all-gather.2 = f32[32,16,8]{1,2,0:T(8,128)S(1)} all-gather(f32[1,16,8]{1,2,0:T(8,128)S(1)} %fusion.10), channel_id=2, replica_groups=mesh['gx'=4,'gy'=2,'gz'=4] {'gx','gy','gz'}, dimensions={0}, use_global_device_ids=true | all-gather | bytes 16896 | tf_op jit(solution)/shard_map/all_gather | solution.py:52
  155.7 1.0 convolution_subtract_fusion
  156.9 0.7 cholesky.105
  159.8 1.0 fusion.64
  160.8 1.3 collective-permute-start.6
  162.1 4.6 %collective-permute-start.7 = (f32[8,1,32,128]{3,0,2,1:T(8,128)S(1)}, f32[8,1,32,128]{3,0,2,1:T(8,128)S(1)}, u32[]{:S(2)}, u32[]{:S(2)}) collective-permute-start(f32[8,1,32,128]{3,0,2,1:T(8,128)S(1)} %get-tuple-element.82), channel_id=1, source_target_pairs={{0,8},{8,16},{16,24},{1,9},{9,17},{17,25},{2,10},{10,18},{18,26},{... | collective-permute-start | bytes 393224 | tf_op jit(solution)/shard_map/ppermute | solution.py:14
  166.7 1.0 collective-permute-done.6
  167.7 1.5 collective-permute-done.7
  169.2 1.3 collective-permute-start.8
  170.5 3.0 %collective-permute-start.9 = (f32[8,10,1,128]{3,0,2,1:T(8,128)S(1)}, f32[8,10,1,128]{3,0,2,1:T(8,128)S(1)}, u32[]{:S(2)}, u32[]{:S(2)}) collective-permute-start(f32[8,10,1,128]{3,0,2,1:T(8,128)S(1)} %get-tuple-element.78), channel_id=1, source_target_pairs={{0,4},{1,5},{2,6},{3,7},{8,12},{9,13},{10,14},{11,15},{16,20},{17,... | collective-permute-start | bytes 122888 | tf_op jit(solution)/shard_map/ppermute | solution.py:14
  173.6 0.8 collective-permute-done.9
  175.1 1.5 fusion.59
  176.6 2.6 copy.137
  179.3 1.3 collective-permute-start.10
  180.5 1.3 copy.139
  181.8 5.2 %collective-permute-start.11 = (f32[8,10,34,1]{2,0,3,1:T(8,128)}, f32[8,10,34,1]{2,0,3,1:T(8,128)}, u32[]{:S(2)}, u32[]{:S(2)}) collective-permute-start(f32[8,10,34,1]{2,0,3,1:T(8,128)} %copy.139), channel_id=1, source_target_pairs={{0,1},{1,2},{2,3},{4,5},{5,6},{6,7},{8,9},{9,10},{10,11},{12,13},{... | collective-permute-start | bytes 32648 | tf_op jit(solution)/shard_map/ppermute | solution.py:14
  188.7 1.5 copy.138
  190.1 2.6 copy.140
  192.7 3.0 %fusion.20 = f32[8,8,32,128]{3,0,2,1:T(8,128)S(1)} fusion(f32[8,10,34,1]{3,0,2,1:T(8,128)} %copy.140, f32[8,10,1,128]{3,0,2,1:T(8,128)S(1)} %collective-permute-done.8, f32[8,10,1,128]{3,0,2,1:T(8,128)} %copy-done.5, f32[8,1,32,128]{3,0,2,1:T(8,128)} %copy-done.1, f32[8,8,32,128]{3,0,2,1:T(8,128)S(1)} %bitcast.81, f32[8,1,32,128]{3,0,2,1:T(8,128)} %copy-done.2, ...), kind=kLoop, calls=%fused_computation.28 | loop fusion | flops 6553600 | bytes 2594048 | tf_op jit(solution)/shard_map/sub | solution.py:27
  195.7 3.0 %fusion.11 = f32[1,24,8]{1,2,0:T(8,128)S(1)} fusion(f32[8,32768]{1,0:T(8,128)S(1)} %bitcast.86, f32[8,32768]{1,0:T(8,128)S(1)} %fusion.64, f32[8,32768]{1,0:T(8,128)S(1)} %fusion.16), kind=kOutput, calls=%fused_computation.16 | convolution fusion | flops 77070336 | bytes 3146496 | tf_op jit(solution)/shard_map/dot_general | solution.py:36
  198.7 65.0 %all-gather.3 = f32[32,24,8]{1,2,0:T(8,128)S(1)} all-gather(f32[1,24,8]{1,2,0:T(8,128)S(1)} %fusion.11), channel_id=3, replica_groups=mesh['gx'=4,'gy'=2,'gz'=4] {'gx','gy','gz'}, dimensions={0}, use_global_device_ids=true | all-gather | bytes 25344 | tf_op jit(solution)/shard_map/all_gather | solution.py:52
  263.9 0.7 cholesky.116
  266.0 2.0 dynamic-slice_select_fusion
  268.0 1.7 scatter.20
  270.5 1.5 cholesky.41
  273.3 1.2 custom-call.15
  275.2 1.1 fusion.7
  276.9 1.2 copy.144
  (69 shorter events, 13.4 us)
Async XLA Ops:
  0.6 49.5 %copy-start = (f32[8,8,32,128]{3,2,1,0:T(8,128)S(1)}, f32[8,8,32,128]{3,2,1,0:T(8,128)}, u32[]{:S(2)}) copy-start(f32[8,8,32,128]{3,2,1,0:T(8,128)} %param.15) | copy-start | bytes 3145732
  51.7 7.1 %collective-permute-start = (f32[8,1,32,128]{3,0,2,1:T(8,128)S(1)}, f32[8,1,32,128]{3,0,2,1:T(8,128)S(1)}, u32[]{:S(2)}, u32[]{:S(2)}) collective-permute-start(f32[8,1,32,128]{3,0,2,1:T(8,128)S(1)} %get-tuple-element.85), channel_id=1, source_target_pairs={{8,0},{16,8},{24,16},{9,1},{17,9},{25,17},{10,2},{18,10},{26,18},{... | collective-permute-start | bytes 393224 | tf_op jit(solution)/shard_map/ppermute | solution.py:17
  53.0 7.3 %collective-permute-start.1 = (f32[8,1,32,128]{3,0,2,1:T(8,128)S(1)}, f32[8,1,32,128]{3,0,2,1:T(8,128)S(1)}, u32[]{:S(2)}, u32[]{:S(2)}) collective-permute-start(f32[8,1,32,128]{3,0,2,1:T(8,128)S(1)} %get-tuple-element.84), channel_id=1, source_target_pairs={{0,8},{8,16},{16,24},{1,9},{9,17},{17,25},{2,10},{10,18},{18,26},{... | collective-permute-start | bytes 393224 | tf_op jit(solution)/shard_map/ppermute | solution.py:14
  58.8 6.8 %copy-start.3 = (f32[8,1,32,128]{3,0,2,1:T(8,128)}, f32[8,1,32,128]{3,0,2,1:T(8,128)S(1)}, u32[]{:S(2)}) copy-start(f32[8,1,32,128]{3,0,2,1:T(8,128)S(1)} %collective-permute-done) | copy-start | bytes 393220
  60.3 5.3 %copy-start.4 = (f32[8,1,32,128]{3,0,2,1:T(8,128)}, f32[8,1,32,128]{3,0,2,1:T(8,128)S(1)}, u32[]{:S(2)}) copy-start(f32[8,1,32,128]{3,0,2,1:T(8,128)S(1)} %collective-permute-done.1) | copy-start | bytes 393220
  60.3 4.3 %collective-permute-start.2 = (f32[8,10,1,128]{3,0,2,1:T(8,128)S(1)}, f32[8,10,1,128]{3,0,2,1:T(8,128)S(1)}, u32[]{:S(2)}, u32[]{:S(2)}) collective-permute-start(f32[8,10,1,128]{3,0,2,1:T(8,128)S(1)} %get-tuple-element.81), channel_id=1, source_target_pairs={{4,0},{5,1},{6,2},{7,3},{12,8},{13,9},{14,10},{15,11},{20,16},{21,... | collective-permute-start | bytes 122888 | tf_op jit(solution)/shard_map/ppermute | solution.py:17
  61.6 3.9 %collective-permute-start.3 = (f32[8,10,1,128]{3,0,2,1:T(8,128)S(1)}, f32[8,10,1,128]{3,0,2,1:T(8,128)S(1)}, u32[]{:S(2)}, u32[]{:S(2)}) collective-permute-start(f32[8,10,1,128]{3,0,2,1:T(8,128)S(1)} %get-tuple-element.80), channel_id=1, source_target_pairs={{0,4},{1,5},{2,6},{3,7},{8,12},{9,13},{10,14},{11,15},{16,20},{17,... | collective-permute-start | bytes 122888 | tf_op jit(solution)/shard_map/ppermute | solution.py:14
  65.5 0.6 copy-start.6
  67.7 8.5 %copy-start.7 = (f32[8,32,128]{2,1,0:T(8,128)S(1)}, f32[8,32,128]{2,1,0:T(8,128)}, u32[]{:S(2)}) copy-start(f32[8,32,128]{2,1,0:T(8,128)} %param.16) | copy-start | bytes 393220
  69.7 7.2 %collective-permute-start.4 = (f32[8,10,34,1]{2,0,3,1:T(8,128)S(1)}, f32[8,10,34,1]{2,0,3,1:T(8,128)S(1)}, u32[]{:S(2)}, u32[]{:S(2)}) collective-permute-start(f32[8,10,34,1]{2,0,3,1:T(8,128)S(1)} %copy.130), channel_id=1, source_target_pairs={{1,0},{2,1},{3,2},{5,4},{6,5},{7,6},{9,8},{10,9},{11,10},{13,12},{... | collective-permute-start | bytes 32648 | tf_op jit(solution)/shard_map/ppermute | solution.py:17
  71.7 6.2 %collective-permute-start.5 = (f32[8,10,34,1]{2,0,3,1:T(8,128)S(1)}, f32[8,10,34,1]{2,0,3,1:T(8,128)S(1)}, u32[]{:S(2)}, u32[]{:S(2)}) collective-permute-start(f32[8,10,34,1]{2,0,3,1:T(8,128)S(1)} %copy.132), channel_id=1, source_target_pairs={{0,1},{1,2},{2,3},{4,5},{5,6},{6,7},{8,9},{9,10},{10,11},{12,13},{... | collective-permute-start | bytes 32648 | tf_op jit(solution)/shard_map/ppermute | solution.py:14
  160.8 6.9 %collective-permute-start.6 = (f32[8,1,32,128]{3,0,2,1:T(8,128)S(1)}, f32[8,1,32,128]{3,0,2,1:T(8,128)S(1)}, u32[]{:S(2)}, u32[]{:S(2)}) collective-permute-start(f32[8,1,32,128]{3,0,2,1:T(8,128)S(1)} %get-tuple-element.83), channel_id=1, source_target_pairs={{8,0},{16,8},{24,16},{9,1},{17,9},{25,17},{10,2},{18,10},{26,18},{... | collective-permute-start | bytes 393224 | tf_op jit(solution)/shard_map/ppermute | solution.py:17
  162.1 7.1 %collective-permute-start.7 = (f32[8,1,32,128]{3,0,2,1:T(8,128)S(1)}, f32[8,1,32,128]{3,0,2,1:T(8,128)S(1)}, u32[]{:S(2)}, u32[]{:S(2)}) collective-permute-start(f32[8,1,32,128]{3,0,2,1:T(8,128)S(1)} %get-tuple-element.82), channel_id=1, source_target_pairs={{0,8},{8,16},{16,24},{1,9},{9,17},{17,25},{2,10},{10,18},{18,26},{... | collective-permute-start | bytes 393224 | tf_op jit(solution)/shard_map/ppermute | solution.py:14
  167.7 6.7 %copy-start.1 = (f32[8,1,32,128]{3,0,2,1:T(8,128)}, f32[8,1,32,128]{3,0,2,1:T(8,128)S(1)}, u32[]{:S(2)}) copy-start(f32[8,1,32,128]{3,0,2,1:T(8,128)S(1)} %collective-permute-done.6) | copy-start | bytes 393220
  169.2 5.2 %copy-start.2 = (f32[8,1,32,128]{3,0,2,1:T(8,128)}, f32[8,1,32,128]{3,0,2,1:T(8,128)S(1)}, u32[]{:S(2)}) copy-start(f32[8,1,32,128]{3,0,2,1:T(8,128)S(1)} %collective-permute-done.7) | copy-start | bytes 393220
  169.2 4.4 %collective-permute-start.8 = (f32[8,10,1,128]{3,0,2,1:T(8,128)S(1)}, f32[8,10,1,128]{3,0,2,1:T(8,128)S(1)}, u32[]{:S(2)}, u32[]{:S(2)}) collective-permute-start(f32[8,10,1,128]{3,0,2,1:T(8,128)S(1)} %get-tuple-element.79), channel_id=1, source_target_pairs={{4,0},{5,1},{6,2},{7,3},{12,8},{13,9},{14,10},{15,11},{20,16},{21,... | collective-permute-start | bytes 122888 | tf_op jit(solution)/shard_map/ppermute | solution.py:17
  170.5 3.9 %collective-permute-start.9 = (f32[8,10,1,128]{3,0,2,1:T(8,128)S(1)}, f32[8,10,1,128]{3,0,2,1:T(8,128)S(1)}, u32[]{:S(2)}, u32[]{:S(2)}) collective-permute-start(f32[8,10,1,128]{3,0,2,1:T(8,128)S(1)} %get-tuple-element.78), channel_id=1, source_target_pairs={{0,4},{1,5},{2,6},{3,7},{8,12},{9,13},{10,14},{11,15},{16,20},{17,... | collective-permute-start | bytes 122888 | tf_op jit(solution)/shard_map/ppermute | solution.py:14
  174.4 0.6 copy-start.5
  179.3 9.4 %collective-permute-start.10 = (f32[8,10,34,1]{2,0,3,1:T(8,128)}, f32[8,10,34,1]{2,0,3,1:T(8,128)}, u32[]{:S(2)}, u32[]{:S(2)}) collective-permute-start(f32[8,10,34,1]{2,0,3,1:T(8,128)} %copy.137), channel_id=1, source_target_pairs={{1,0},{2,1},{3,2},{5,4},{6,5},{7,6},{9,8},{10,9},{11,10},{13,12},{... | collective-permute-start | bytes 32648 | tf_op jit(solution)/shard_map/ppermute | solution.py:17
  181.8 8.3 %collective-permute-start.11 = (f32[8,10,34,1]{2,0,3,1:T(8,128)}, f32[8,10,34,1]{2,0,3,1:T(8,128)}, u32[]{:S(2)}, u32[]{:S(2)}) collective-permute-start(f32[8,10,34,1]{2,0,3,1:T(8,128)} %copy.139), channel_id=1, source_target_pairs={{0,1},{1,2},{2,3},{4,5},{5,6},{6,7},{8,9},{9,10},{10,11},{12,13},{... | collective-permute-start | bytes 32648 | tf_op jit(solution)/shard_map/ppermute | solution.py:14
